TPU v7x, 128 devices: a whole 4x4x4 slice. The times are simulated.
128 devices in a mesh: dp: 1, tp: 128 (over z, y, x, core).
Axes of the slice: x: 4, y: 4, z: 4, core: 2. Of those that a mesh axis runs over, the one named last changes fastest.
Arguments:
- hidden: bfloat16 [384, 3, 2048], P(('dp', 'tp'))
- w_head: bfloat16 [2048, 128256], P(None, 'tp')
- q_draft: float32 [384, 2, 128256], P(('dp', 'tp'))
- draft_tok: int32 [384, 2], P('dp')
Outputs:
- output 1: float32 [384, 2], P('dp')
- output 2: float32 [384], P('dp')
- output 3: float32 [384, 2, 128256], P('dp', None, 'tp')
- output 4: float32 [384, 128256], P('dp', 'tp')
All inputs are finite; a program needn't handle non-finite values.
Results may differ from a plain program's by a relative error of at most 0.001.
Values are sent between devices in bfloat16 or wider.
A program may use at most 1 GiB of HBM per device.

v0:
```python
import jax
import jax.numpy as jnp
from jax import lax
from jax.sharding import PartitionSpec as P

INV_TEMP = 1.25


def verify_local(hid_rows, w_cols, q_rows, draft_tok):
    shard_vocab = w_cols.shape[1]
    hid_all = lax.all_gather(hid_rows, 'tp', axis=0, tiled=True)
    logits = jnp.einsum('bgd,dv->bgv', hid_all, w_cols, preferred_element_type=jnp.float32) * INV_TEMP
    glob_max = lax.pmax(jnp.max(logits, axis=-1, keepdims=True), 'tp')
    exp_terms = jnp.exp(logits - glob_max)
    exp_total = lax.psum(jnp.sum(exp_terms, axis=-1, keepdims=True), 'tp')
    target_prob = exp_terms / exp_total
    draft_part = target_prob[:, :-1]
    q_cols = lax.all_to_all(q_rows, 'tp', 2, 0, tiled=True)
    local_ids = draft_tok - lax.axis_index('tp') * shard_vocab
    picker = local_ids[:, :, None] == jnp.arange(shard_vocab, dtype=jnp.int32)
    p_pick = jnp.sum(jnp.where(picker, draft_part, 0.0), axis=-1)
    q_pick = jnp.sum(jnp.where(picker, q_cols, 0.0), axis=-1)
    pick_pair = lax.psum(jnp.stack([p_pick, q_pick]), 'tp')
    accept = jnp.minimum(pick_pair[0] / pick_pair[1], 1.0)
    expected = jnp.sum(jnp.cumprod(accept, axis=1), axis=1)
    excess = jnp.maximum(draft_part - q_cols, 0.0)
    excess_mass = lax.psum(jnp.sum(excess, axis=-1, keepdims=True), 'tp')
    return accept, expected, excess / excess_mass, target_prob[:, -1]


def solution(mesh):
    return jax.shard_map(
        verify_local,
        mesh=mesh,
        in_specs=(P(('dp', 'tp'), None, None), P(None, 'tp'), P(('dp', 'tp'), None, None), P('dp', None)),
        out_specs=(P('dp', None), P('dp'), P('dp', None, 'tp'), P('dp', 'tp')),
        check_vma=False,
    )
```

profile of v0, /device:TPU:1, one launch (start us, length us, event | category | flops | bytes accessed | tf_op | source)
XLA Modules:
  0.0 858.3 jit_solution(450575986026121736)
XLA Ops:
  7.2 0.7 all-gather.2.cloned.1.call-update
  7.9 123.6 %copy.26 = f32[3,2,128256]{0,1,2:T(2,128)} copy(f32[3,2,128256]{2,1,0:T(2,128)} %param.6) | data formatting | bytes 6156288 | tf_op args[2]
  131.5 159.3 %reshape.19 = f32[128,1,6012]{2,1,0:T(1,128)} reshape(f32[128256,2,3]{2,1,0:T(2,128)} %bitcast.16) | data formatting | bytes 6156288
  290.8 11.5 %all-to-all-start = ((f32[128,1,6012]{2,1,0:T(1,128)}), f32[128,1,6012]{2,1,0:T(1,128)S(1)}, u32[]{:S(2)}, u32[]{:S(2)}) async-start(f32[128,1,6012]{2,1,0:T(1,128)} %reshape.19), calls=%async_computation | async-start | bytes 6160384 | tf_op jit(solution)/shard_map/all_to_all | solution.py:18
  302.6 42.2 %all-to-all-done = f32[128,1,6012]{2,1,0:T(1,128)S(1)} async-done(((f32[128,1,6012]{2,1,0:T(1,128)}), f32[128,1,6012]{2,1,0:T(1,128)S(1)}, u32[]{:S(2)}, u32[]{:S(2)}) %all-to-all-start) | async-done | bytes 3078176 | tf_op jit(solution)/shard_map/all_to_all | solution.py:18
  344.8 1.6 copy-done.1
  347.0 9.8 %reduce.1 = f32[128,6012]{1,0:T(8,128)S(1)} reduce(f32[128,1,6012]{2,1,0:T(1,128)} %copy-done.1, f32[]{:T(128)} %broadcast.6), dimensions={1}, to_apply=%all_to_all.13.reduce_sub_computation | reduce | bytes 6156292 | tf_op jit(solution)/shard_map/all_to_all | solution.py:18
  356.8 155.9 %reshape.20 = f32[128256,2,3]{2,1,0:T(2,128)} reshape(f32[128,6012]{1,0:T(8,128)S(1)} %reduce.1) | data formatting | bytes 6156288
  512.7 104.5 %copy.32 = f32[3,2,128,1002]{3,2,1,0:T(8,128)S(1)} copy(f32[3,2,128,1002]{0,1,3,2:T(2,128)} %bitcast.2) | data formatting | bytes 6156288 | tf_op jit(solution)/shard_map/all_to_all | solution.py:18
  617.2 0.6 select_reduce_fusion
  618.1 4.1 copy.29
  622.2 4.5 copy.30
  626.7 17.8 %multiply_reduce_fusion = (f32[384,3]{0,1:T(4,128)S(1)}, f32[384,3,1002]{0,2,1:T(8,128)}) fusion(bf16[2048,1002]{0,1:T(8,128)(2,1)} %param.5, bf16[384,3,2048]{2,1,0:T(4,128)(2,1)} %all-gather.2.cloned.1.call-done), kind=kOutput, calls=%fused_computation.3 | convolution fusion | flops 4730336256 | bytes 13444608 | tf_op jit(solution)/shard_map/bgd,dv->bgv/dot_general | solution.py:12
  644.6 65.0 %pmax.7 = f32[384,3]{0,1:T(4,128)S(1)} all-reduce(f32[384,3]{0,1:T(4,128)S(1)} %get-tuple-element.24), channel_id=1, replica_groups=mesh['dp'=1,'tp'=128] {'tp'}, use_global_device_ids=true, to_apply=%region_1.0 | all-reduce | flops 1152 | bytes 9216 | tf_op jit(solution)/shard_map/pmax | solution.py:13
  709.6 3.1 fusion.4
  712.7 64.2 %psum.21 = f32[384,3]{0,1:T(4,128)S(1)} all-reduce(f32[384,3]{0,1:T(4,128)S(1)} %fusion.4), channel_id=1, replica_groups=mesh['dp'=1,'tp'=128] {'tp'}, use_global_device_ids=true, to_apply=%region_3.0 | all-reduce | flops 1152 | bytes 9216 | tf_op jit(solution)/shard_map/psum | solution.py:15
  776.8 3.1 fusion.3
  779.9 1.3 slice_bitcast_fusion
  781.2 0.7 fusion.5
  781.9 0.6 copy-done
  782.5 62.8 %all-reduce = (f32[2,384,2]{1,2,0:T(2,128)S(1)}, f32[384,2]{0,1:T(2,128)S(1)}) all-reduce(f32[2,384,2]{1,2,0:T(2,128)S(1)} %pad_maximum_fusion, f32[384,2]{0,1:T(2,128)S(1)} %get-tuple-element.20), channel_id=1, replica_groups=mesh['dp'=1,'tp'=128] {'tp'}, use_global_device_ids=true, to_apply=%region_6.7 | all-reduce | flops 2304 | bytes 18432 | tf_op jit(solution)/shard_map/psum | solution.py:23
  845.4 2.2 broadcast_divide_fusion
  847.6 3.2 copy.31
  850.8 0.6 reduce_sum.48
  (17 shorter events, 1.3 us)
Async XLA Ops:
  7.2 619.6 %all-gather.2.cloned.1.call-start = ((), (), s32[]{:S(2)}) async-start(), calls=%async_computation.1 | async-start | bytes 6340608 | tf_op jit(solution)/shard_map/all_gather | solution.py:11
  290.8 11.5 %copy-start.3 = (s32[384,2]{0,1:T(2,128)S(1)}, s32[384,2]{0,1:T(2,128)}, u32[]{:S(2)}) copy-start(s32[384,2]{0,1:T(2,128)} %param.7) | copy-start | bytes 9220
  290.8 54.0 %all-to-all-start = ((f32[128,1,6012]{2,1,0:T(1,128)}), f32[128,1,6012]{2,1,0:T(1,128)S(1)}, u32[]{:S(2)}, u32[]{:S(2)}) async-start(f32[128,1,6012]{2,1,0:T(1,128)} %reshape.19), calls=%async_computation | async-start | bytes 6160384 | tf_op jit(solution)/shard_map/all_to_all | solution.py:18
  344.8 1.6 copy-start.1
  779.9 2.6 copy-start
  845.4 5.4 copy-start.2
Sparse Core Ops, SparseCore 0:
  11.1 71.8 all-gather.1
where the time goes:
time: 873 us; the launch traced here: 858 us
  local copies, waits for them, and re-layouts  560 us (64%)
  blocking collectives  192 us (22%)
  waiting for transfers between devices  42.9 us (5%)
  other arithmetic  20.1 us (2%)
  matrix products  17.8 us (2%)
  between operations  14.1 us (2%)
  starting transfers between devices  11.5 us (1%)
    unnamed x12, local copies, waits for them, and re-layouts  444 us
    all_to_all x4, local copies, waits for them, and re-layouts, verify_local(): q_cols = lax.all_to_all(q_rows, 'tp', 2, 0, tiled=True)  114 us
    pmax x1, blocking collectives, verify_local(): glob_max = lax.pmax(jnp.max(logits, axis=-1, keepdims=True), 'tp')  65 us
    psum x1, blocking collectives, verify_local(): exp_total = lax.psum(jnp.sum(exp_terms, axis=-1, keepdims=True), 'tp')  64.2 us
    psum x1, blocking collectives, verify_local(): pick_pair = lax.psum(jnp.stack([p_pick, q_pick]), 'tp')  62.8 us
    all_to_all x1, waiting for transfers between devices, verify_local(): q_cols = lax.all_to_all(q_rows, 'tp', 2, 0, tiled=True)  42.2 us
    dot_general x1, matrix products, verify_local(): jnp.einsum('bgd,dv->bgv', hid_all, w_cols, preferred_element_type=jnp.flo...  17.8 us
  transfers between devices with their start and end apart: 2, of which 1 were waited for; matrix products, arithmetic and copies ran while one was open for 66% of the time, Pallas kernels for 0%

commit v1 on v0

v1 whole, which is shorter than its diff:
```python
import jax
import jax.numpy as jnp
from jax import lax
from jax.experimental import pallas as pl
from jax.experimental.layout import Layout, with_layout_constraint
from jax.experimental.pallas import tpu as pltpu
from jax.sharding import PartitionSpec as P

INV_TEMP = 1.25
DEV = 128
SEQ = 3
NPOS = 3
DRAFT = 2
BATCH = 384
DIM = 2048
VOCAB = 128256
SHARD = VOCAB // DEV
LANES = 128
TILES = VOCAB // LANES
CHUNKS = 8
TAIL = SHARD - (CHUNKS - 1) * LANES
ROWS_P = 1008
TAIL_P = ROWS_P - (CHUNKS - 1) * LANES
KC = DIM // LANES
HROWS = SEQ * NPOS * KC
COLS = NPOS * BATCH
COLS_P = 1280
CT = COLS // LANES
BT = BATCH // LANES
BLK = SEQ * CHUNKS
PITCH = 49
NEG = -1e30
STAT = 24
MESH = pl.DeviceIdType.MESH


def remote(src, dst, ssem, rsem, dev):
    return pltpu.make_async_remote_copy(
        src_ref=src, dst_ref=dst, send_sem=ssem, recv_sem=rsem,
        device_id={'tp': dev}, device_id_type=MESH)


def reduce_round(me, bufa, bufb, sa, ra, sb, rb, payload, combine):
    slot, grp = me % 8, me // 8
    bufa[slot] = payload
    copies = []
    for r in range(1, 8):
        cp = remote(bufa.at[slot], bufa.at[slot], sa.at[r - 1], ra.at[r - 1], grp * 8 + (slot + r) % 8)
        cp.start()
        copies.append(cp)
    for cp in copies:
        cp.wait()
    bufb[grp] = combine([bufa[k] for k in range(8)])
    copies = []
    for r in range(1, 16):
        cp = remote(bufb.at[grp], bufb.at[grp], sb.at[r - 1], rb.at[r - 1], ((grp + r) % 16) * 8 + slot)
        cp.start()
        copies.append(cp)
    for cp in copies:
        cp.wait()
    return combine([bufb[k] for k in range(16)])


def merge_max_sum(parts):
    m = parts[0][0:CT]
    for p in parts[1:]:
        m = jnp.maximum(m, p[0:CT])
    s = parts[0][CT:2 * CT] * jnp.exp(parts[0][0:CT] - m)
    for p in parts[1:]:
        s = s + p[CT:2 * CT] * jnp.exp(p[0:CT] - m)
    return jnp.concatenate([m, s, jnp.zeros((STAT - 2 * CT, LANES), jnp.float32)], axis=0)


def merge_add(parts):
    total = parts[0]
    for p in parts[1:]:
        total = total + p
    return total


def kernel(q_hbm, w_hbm, h_ref, tok_ref,
           ex_hbm, bo_hbm, fac_ref, mass_ref, acc_ref,
           qbuf, wbuf, hidb, bounce, hmat, z, send, recv, exbuf, stat, scale,
           a1, b1, a2, b2,
           lsem, ag_s, ag_r, d2d_s, d2d_r, qs_sem, qr_sem,
           sa1, ra1, sb1, rb1, sa2, ra2, sb2, rb2):
    me = lax.axis_index('tp')
    core = me % 2
    coord = (me // 32, (me // 8) % 4, (me // 2) % 4)

    qcp = pltpu.make_async_copy(q_hbm, qbuf.at[pl.ds(0, SEQ * TILES * DRAFT)], lsem.at[0])
    qcp.start()
    wcp = pltpu.make_async_copy(w_hbm, wbuf, lsem.at[1])
    wcp.start()
    hview = hidb.reshape(4, 4, 4, 2, SEQ, HROWS // SEQ, LANES)
    own = hview.at[coord[0], coord[1], coord[2], core]
    hcp = pltpu.make_async_copy(h_ref.reshape(SEQ, HROWS // SEQ, LANES), own, lsem.at[2])
    hcp.start()
    hcp.wait()

    def sel(j, phase):
        order = [(j + k) % 3 for k in range(3)]
        idx = [coord[0], coord[1], coord[2]]
        for d in order[:phase]:
            idx[d] = slice(None)
        return hview.at[idx[0], idx[1], idx[2], core, j], order[phase]

    def ag_phase(phase):
        out = []
        for j in range(3):
            view, dim = sel(j, phase)
            for r in (1, 3, 2):
                to = list(coord)
                to[dim] = (coord[dim] + r) % 4
                dev = ((to[0] * 4 + to[1]) * 4 + to[2]) * 2 + core
                cp = remote(view, view, ag_s.at[phase, j, r - 1], ag_r.at[phase, j, r - 1], dev)
                cp.start()
                out.append(cp)
        return out

    qrows = qbuf.reshape(qbuf.shape[0], LANES)
    lane = lax.broadcasted_iota(jnp.int32, (8, LANES), 1)

    def pack(k, carry):
        first = (SHARD * k) // LANES
        off = (SHARD * k) % LANES
        shift = (LANES - off) % LANES
        keep = lane < LANES - off
        for i in range(DRAFT):
            for s in range(SEQ):
                base = (s * TILES + first) * DRAFT + i
                lo = qrows[pl.ds(base, 8, stride=2), :]
                hi = qrows[pl.ds(base + 2, 8, stride=2), :]
                lo = pltpu.roll(lo, shift, 1)
                hi = pltpu.roll(hi, shift, 1)
                send[i, pl.ds(pl.multiple_of(k * BLK + s * 8, 8), 8), :] = jnp.where(keep, lo, hi)
        return carry

    c0 = ag_phase(0)
    qcp.wait()
    lax.fori_loop(0, DEV, pack, 0)
    for cp in c0:
        cp.wait_recv()
    c1 = ag_phase(1)
    for cp in c1:
        cp.wait_recv()
    c2 = ag_phase(2)

    def exchange(i):
        pltpu.make_async_copy(
            send.at[i, pl.ds(pl.multiple_of(me * BLK, 8), BLK)],
            recv.at[i, pl.ds(pl.multiple_of(me * BLK, 8), BLK)], qr_sem.at[i]).start()

        def one(n, carry):
            r = (n * 37) % DEV
            rz, ry, rx, rc = r // 32, (r // 8) % 4, (r // 2) % 4, r % 2
            dev = ((((coord[0] + rz) % 4) * 4 + (coord[1] + ry) % 4) * 4 + (coord[2] + rx) % 4) * 2 + (core + rc) % 2
            remote(send.at[i, pl.ds(pl.multiple_of(dev * BLK, 8), BLK)],
                   recv.at[i, pl.ds(pl.multiple_of(me * BLK, 8), BLK)],
                   qs_sem.at[i], qr_sem.at[i], dev).start()
            return carry

        lax.fori_loop(1, DEV, one, 0)

    exchange(0)

    d2d = []
    for j in range(3):
        for cp in c2[3 * j:3 * j + 3]:
            cp.wait_recv()
        view = hview.at[:, :, :, core, j]
        cp = remote(view, view, d2d_s.at[j], d2d_r.at[j], me - core + 1 - core)
        cp.start()
        d2d.append(cp)
    for cp in d2d:
        cp.wait_recv()
    for cp in c0 + c1 + c2 + d2d:
        cp.wait_send()

    def relayout(n, carry):
        def up(b, c):
            x = hidb[pl.ds(pl.multiple_of((48 * n + b) * 48, 16), 48), :]
            bounce[pl.ds(b * PITCH, 48), :] = x.astype(jnp.float32)
            return c

        lax.fori_loop(0, 48, up, 0, unroll=4)
        for g in range(NPOS):
            for u in range(3):
                for kc in range(KC):
                    y = bounce[pl.ds(16 * u * PITCH + g * KC + kc, 16, stride=PITCH), :]
                    hmat[pl.ds(pl.multiple_of(g * BATCH + 48 * n + 16 * u, 16), 16),
                         kc * LANES:(kc + 1) * LANES] = y.astype(jnp.bfloat16)
        return carry

    lax.fori_loop(0, 8, relayout, 0)
    wcp.wait()

    z[SHARD:ROWS_P, :] = jnp.full((ROWS_P - SHARD, COLS_P), NEG, jnp.float32)

    def head(n, carry):
        hb = hmat[pl.ds(pl.multiple_of(n * 256, 256), 256), :]
        zt = lax.dot_general(wbuf[...], hb, (((1,), (1,)), ((), ())), preferred_element_type=jnp.float32)
        z[0:SHARD, pl.ds(pl.multiple_of(n * 256, 256), 256)] = zt * INV_TEMP
        return carry

    lax.fori_loop(0, COLS_P // 256, head, 0)

    def local_stats(t, carry):
        cols = pl.ds(pl.multiple_of(t * LANES, LANES), LANES)

        def peak(n, m):
            x = z[pl.ds(pl.multiple_of(n * 112, 8), 112), cols]
            return jnp.maximum(m, jnp.max(x.reshape(14, 8, LANES), axis=0))

        m8 = lax.fori_loop(0, 9, peak, jnp.full((8, LANES), NEG, jnp.float32))
        m = jnp.max(m8, axis=0, keepdims=True)

        def expo(n, s):
            rows = pl.ds(pl.multiple_of(n * 112, 8), 112)
            x = jnp.exp(z[rows, cols] - m)
            z[rows, cols] = x
            return s + jnp.sum(x.reshape(14, 8, LANES), axis=0)

        s8 = lax.fori_loop(0, 9, expo, jnp.zeros((8, LANES), jnp.float32))
        stat[pl.ds(t, 1), :] = m
        stat[pl.ds(CT + t, 1), :] = jnp.sum(s8, axis=0, keepdims=True)
        return carry

    stat[...] = jnp.zeros_like(stat)
    lax.fori_loop(0, CT, local_stats, 0)
    bcp = pltpu.make_async_copy(z.at[:, DRAFT * BATCH:COLS], bo_hbm, lsem.at[2])
    bcp.start()

    local = stat[...]
    tot = reduce_round(me, a1, b1, sa1, ra1, sb1, rb1, local, merge_max_sum)
    exchange(1)
    fac = jnp.exp(local[0:CT] - tot[0:CT]) / tot[CT:2 * CT]
    scale[0:CT, :] = fac
    for t in range(BT):
        fac_ref[0:1, t * LANES:(t + 1) * LANES] = fac[DRAFT * BT + t:DRAFT * BT + t + 1]

    exrows = exbuf.reshape(exbuf.shape[0], LANES)
    first_id = me * SHARD
    stat[...] = jnp.zeros_like(stat)
    for i in range(DRAFT):
        pltpu.make_async_copy(recv.at[i], recv.at[i], qr_sem.at[i]).wait()
        for t in range(BT):
            row = i * BT + t
            sc = scale[row:row + 1, :]
            tok = tok_ref[i:i + 1, t * LANES:(t + 1) * LANES] - first_id
            col0 = i * BATCH + t * LANES

            def block(c, carry, size, valid):
                mass, pp, qp = carry
                q = recv[i, pl.ds(t * LANES * CHUNKS + c, LANES, stride=CHUNKS), :].T
                p = z[pl.ds(pl.multiple_of(c * LANES, LANES), size), col0:col0 + LANES] * sc
                ids = lax.broadcasted_iota(jnp.int32, (size, LANES), 0)
                q = q[0:size]
                if valid < size:
                    q = jnp.where(ids < valid, q, 0.0)
                x = jnp.maximum(p - q, 0.0)
                exrows[pl.ds(c * LANES * 6 + t * 2 + i, valid, stride=6), :] = x[0:valid]
                hit = ids == tok - c * LANES
                fold = lambda v: jnp.sum(v.reshape(size // 8, 8, LANES), axis=0)
                return (mass + fold(x), pp + fold(jnp.where(hit, p, 0.0)), qp + fold(jnp.where(hit, q, 0.0)))

            zero = jnp.zeros((8, LANES), jnp.float32)
            carry = lax.fori_loop(0, CHUNKS - 1, lambda c, v: block(c, v, LANES, LANES), (zero, zero, zero))
            mass, pp, qp = block(CHUNKS - 1, carry, TAIL_P, TAIL)
            stat[row:row + 1, :] = jnp.sum(mass, axis=0, keepdims=True)
            stat[6 + row:7 + row, :] = jnp.sum(pp, axis=0, keepdims=True)
            stat[12 + row:13 + row, :] = jnp.sum(qp, axis=0, keepdims=True)

    ecp = pltpu.make_async_copy(exbuf, ex_hbm, lsem.at[0])
    ecp.start()
    tot = reduce_round(me, a2, b2, sa2, ra2, sb2, rb2, stat[...], merge_add)
    acc = jnp.minimum(tot[6:12] / tot[12:18], 1.0)
    for i in range(DRAFT):
        for t in range(BT):
            row = i * BT + t
            mass_ref[i:i + 1, t * LANES:(t + 1) * LANES] = tot[row:row + 1]
            acc_ref[i:i + 1, t * LANES:(t + 1) * LANES] = acc[row:row + 1]
    ecp.wait()
    bcp.wait()
    for i in range(DRAFT):
        part = send.at[i, pl.ds(0, (DEV - 1) * BLK)]
        pltpu.make_async_copy(part, part, qs_sem.at[i]).wait()


def verify_local(hid, w_cols, q_rows, draft_tok):
    q = with_layout_constraint(q_rows.reshape(SEQ, DRAFT, TILES, LANES), Layout((0, 2, 1, 3)))
    q = q.transpose(0, 2, 1, 3).reshape(SEQ * TILES * DRAFT, 1, LANES)
    f32 = jnp.float32
    hbm = pl.BlockSpec(memory_space=pl.ANY)
    vmem = pl.BlockSpec(memory_space=pltpu.VMEM)
    dma = pltpu.SemaphoreType.DMA
    ex, bo, fac, mass, acc = pl.pallas_call(
        kernel,
        out_shape=[
            jax.ShapeDtypeStruct((SHARD * BT * DRAFT, 1, LANES), f32),
            jax.ShapeDtypeStruct((ROWS_P, BATCH), f32),
            jax.ShapeDtypeStruct((1, BATCH), f32),
            jax.ShapeDtypeStruct((DRAFT, BATCH), f32),
            jax.ShapeDtypeStruct((DRAFT, BATCH), f32),
        ],
        in_specs=[hbm, hbm, vmem, vmem],
        out_specs=[hbm, hbm, vmem, vmem, vmem],
        scratch_shapes=[
            pltpu.VMEM((SEQ * TILES * DRAFT + 20, 1, LANES), f32),
            pltpu.VMEM((SHARD, DIM), jnp.bfloat16),
            pltpu.VMEM((DEV * HROWS, LANES), jnp.bfloat16),
            pltpu.VMEM((48 * PITCH, LANES), f32),
            pltpu.VMEM((COLS_P, DIM), jnp.bfloat16),
            pltpu.VMEM((ROWS_P, COLS_P), f32),
            pltpu.VMEM((DRAFT, DEV * BLK, LANES), f32),
            pltpu.VMEM((DRAFT, DEV * BLK, LANES), f32),
            pltpu.VMEM((SHARD * BT * DRAFT, 1, LANES), f32),
            pltpu.VMEM((STAT, LANES), f32),
            pltpu.VMEM((16, LANES), f32),
            pltpu.VMEM((8, STAT, LANES), f32),
            pltpu.VMEM((16, STAT, LANES), f32),
            pltpu.VMEM((8, STAT, LANES), f32),
            pltpu.VMEM((16, STAT, LANES), f32),
            dma((3,)),
            dma((3, 3, 3)), dma((3, 3, 3)), dma((3,)), dma((3,)),
            dma((2,)), dma((2,)),
            dma((7,)), dma((7,)), dma((15,)), dma((15,)),
            dma((7,)), dma((7,)), dma((15,)), dma((15,)),
        ],
        compiler_params=pltpu.CompilerParams(vmem_limit_bytes=62 * 2 ** 20, has_side_effects=True),
    )(q, w_cols.T, hid.reshape(HROWS, LANES), draft_tok.T)
    ex = with_layout_constraint(ex.reshape(SHARD, BT, DRAFT, LANES).transpose(0, 2, 1, 3), Layout((0, 2, 1, 3)))
    residual = (ex.reshape(SHARD, DRAFT, BATCH) / mass[None]).transpose(2, 1, 0)
    bonus = (bo[:SHARD] * fac).T
    expected = acc[0] * (1.0 + acc[1])
    return acc.T, expected, residual, bonus


def solution(mesh):
    return jax.shard_map(
        verify_local,
        mesh=mesh,
        in_specs=(P(('dp', 'tp'), None, None), P(None, 'tp'), P(('dp', 'tp'), None, None), P('dp', None)),
        out_specs=(P('dp', None), P('dp'), P('dp', None, 'tp'), P('dp', 'tp')),
        check_vma=False,
    )
```

time: 873 us -> 127 us (0.15); the launches traced: 858 us -> 126 us
  local copies, waits for them, and re-layouts: 560 us -> 2.06 us
  blocking collectives: 192 us -> 0 us
  Pallas kernels: 0 us -> 117 us
  waiting for transfers between devices: 42.9 us -> 0 us
  matrix products: 17.8 us -> 0 us
  between operations: 14.1 us -> 0.66 us
  other arithmetic: 20.1 us -> 6.84 us
  starting transfers between devices: 11.5 us -> 0 us
    unnamed x12 -> x7, local copies, waits for them, and re-layouts: 444 us -> 0.59 us
    psum x2 -> x0, blocking collectives: 127 us -> none  [the longest x1 64.2 us: verify_local(): exp_total = lax.psum(jnp.sum(exp_terms, axis=-1, keepdims=True), 'tp')]
    pallas_call x0 -> x1, Pallas kernels: none -> 117 us  [verify_local(): pl.pallas_call(kernel, out_shape=[jax.ShapeDtypeStruct((SHARD * BT * DRAF...]
    all_to_all x4 -> x0, local copies, waits for them, and re-layouts: 114 us -> none  [verify_local(): q_cols = lax.all_to_all(q_rows, 'tp', 2, 0, tiled=True)]
    pmax x1 -> x0, blocking collectives: 65 us -> none  [verify_local(): glob_max = lax.pmax(jnp.max(logits, axis=-1, keepdims=True), 'tp')]
    all_to_all x1 -> x0, waiting for transfers between devices: 42.2 us -> none  [verify_local(): q_cols = lax.all_to_all(q_rows, 'tp', 2, 0, tiled=True)]
    dot_general x1 -> x0, matrix products: 17.8 us -> none  [verify_local(): jnp.einsum('bgd,dv->bgv', hid_all, w_cols, preferred_element_type=jnp.flo...]
    all_to_all x1 -> x0, starting transfers between devices: 11.5 us -> none  [verify_local(): q_cols = lax.all_to_all(q_rows, 'tp', 2, 0, tiled=True)]
  transfers between devices with their start and end apart: 2 -> 0, of which waited for: 1 -> 0; matrix products, arithmetic and copies ran while one was open for 66% -> 0% of each run, Pallas kernels for 0% -> 0%
where the time goes in v1:
time: 127 us; the launch traced here: 126 us
  Pallas kernels  117 us (92%)
  other arithmetic  6.84 us (5%)
  local copies, waits for them, and re-layouts  2.06 us (2%)
    pallas_call x1, Pallas kernels, verify_local(): pl.pallas_call(kernel, out_shape=[jax.ShapeDtypeStruct((SHARD * BT * DRAF...  117 us
    transpose x1, other arithmetic, verify_local(): bonus = (bo[:SHARD] * fac).T  2.71 us
    transpose x1, other arithmetic, verify_local(): residual = (ex.reshape(SHARD, DRAFT, BATCH) / mass[None]).transpose(2, 1, 0)  2.7 us

profile of v1, /device:TPU:1, one launch (start us, length us, event | category | flops | bytes accessed | tf_op | source)
XLA Modules:
  0.0 126.2 jit_solution(16354430121355671738)
XLA Ops:
  0.6 1.5 %reshape.29.h_ref = bf16[144,128]{1,0:T(8,128)(2,1)} reshape(bf16[3,3,2048]{2,1,0:T(4,128)(2,1)} %param.4) | data formatting | bytes 73728 | tf_op jit(solution)/shard_map/reshape | solution.py:331
  2.1 116.6 %shard_map.75 = (f32[6012,1,128]{2,1,0:T(1,128)}, f32[1008,384]{1,0:T(8,128)}, f32[1,384]{1,0:T(1,128)}, f32[2,384]{1,0:T(2,128)}, f32[2,384]{1,0:T(2,128)}) custom-call(f32[6012,1,128]{2,1,0:T(1,128)} %bitcast.18, bf16[1002,2048]{1,0:T(8,128)(2,1)} %bitcast.17, bf16[144,128]{1,0:T(8,128)(2,1)} %reshape.29.h_ref, s32[2,384]{1,0:T(2,128)} %bitcast.21), custom_call_target="tpu_custom_call" | custom-call | tf_op jit(solution)/shard_map/pallas_call | solution.py:297
  118.7 0.0 copy-start
  118.8 0.0 copy-start.2
  118.8 0.8 reduce.1
  119.6 2.7 %multiply_bitcast_fusion = f32[384,1002]{0,1:T(8,128)} fusion(f32[1008,384]{1,0:T(8,128)} %get-tuple-element.12, f32[384]{0:T(512)S(1)} %reduce.1), kind=kLoop, calls=%fused_computation.1 | loop fusion | flops 384768 | bytes 3079680 | tf_op jit(solution)/shard_map/transpose | solution.py:334
  122.3 0.0 copy-done
  122.3 0.0 copy-done.2
  122.3 0.0 copy-start.1
  122.3 2.7 %divide_bitcast_fusion = f32[384,2,1002]{0,1,2:T(2,128)} fusion(f32[1002,2,384]{2,1,0:T(2,128)S(1)} %bitcast.19, f32[2,384]{1,0:T(2,128)S(1)} %copy-done.2), kind=kLoop, calls=%fused_computation | loop fusion | flops 769536 | bytes 6159360 | tf_op jit(solution)/shard_map/transpose | solution.py:333
  125.0 0.0 copy-done.1
  125.0 0.6 multiply_reduce_fusion
  125.6 0.6 copy.9
Async XLA Ops:
  118.7 3.6 %copy-start = (f32[6012,1,128]{2,1,0:T(1,128)S(1)}, f32[6012,1,128]{2,1,0:T(1,128)}, u32[]{:S(2)}) copy-start(f32[6012,1,128]{2,1,0:T(1,128)} %get-tuple-element.10) | copy-start | bytes 9234436
  118.8 3.6 %copy-start.2 = (f32[2,384]{1,0:T(2,128)S(1)}, f32[2,384]{1,0:T(2,128)}, u32[]{:S(2)}) copy-start(f32[2,384]{1,0:T(2,128)} %get-tuple-element.11) | copy-start | bytes 9220
  122.3 2.7 %copy-start.1 = (f32[2,384]{1,0:T(2,128)S(1)}, f32[2,384]{1,0:T(2,128)}, u32[]{:S(2)}) copy-start(f32[2,384]{1,0:T(2,128)} %get-tuple-element.9) | copy-start | bytes 9220
